TPU v7x, 32 devices: a whole 2x2x4 slice. The times are simulated.
32 devices in a mesh: layer: 4 (over y, core), col: 4 (over z), row: 2 (over x).
Axes of the slice: x: 2, y: 2, z: 4, core: 2. Of those that a mesh axis runs over, the one named last changes fastest.
Arguments:
- activations: bfloat16 [4, 768, 4096], P(None, ('layer', 'row'), 'col'), may hold values from -6 to 6
- out_grads: bfloat16 [4, 768, 11008], P(None, ('layer', 'col'), 'row'), may hold values from -0.02734375 to 0.02734375
- basis_in: bfloat16 [4, 4096, 4096], P('layer', 'col', 'row'), may hold values from -0.09375 to 0.09375
- basis_out: bfloat16 [4, 11008, 11008], P('layer', 'row', 'col'), may hold values from -0.0546875 to 0.0546875
- eigenvalues: float32 [4, 11008, 4096], P('layer', 'col', 'row'), may hold values from 0.01 to 10
- damping: float32 [4], P('layer'), may hold values from 0.05 to 0.5
- layer_order: int32 [4], replicated, may hold values from 0 to 3, each once
- query_ids: int32 [256], replicated, may hold values from 0 to 3, never falling along the last dimension, each value on 1 to 128 neighbouring positions
- train_ids: int32 [512], replicated, may hold values from 0 to 15, never falling along the last dimension, each value on 1 to 64 neighbouring positions
Outputs:
- scores: float32 [4, 16], replicated
Inputs may be any that keep to these rules, and one draw needn't show every extreme that they name: `layer_order`: each slot's layer appears once. `query_ids`: never falling; every query example has 1 to 128 tokens. `train_ids`: never falling; every train example has 1 to 64 tokens.
All inputs are finite; a program needn't handle non-finite values.
Results may differ from a plain program's by a relative error of at most 0.02.
Values may be sent and summed in bfloat16 or wider, within the bound.
No kernel may reach another device: no remote copies, remote signals or barrier semaphores. Data moves between devices by JAX's collectives and lax.ppermute only.
A program may use at most 192 MiB of HBM per device.

v0:
```python
import jax
import jax.numpy as jnp
from jax import lax
from jax.sharding import PartitionSpec as P

QUERIES = 4
TRAIN = 16


def body(
    activations,
    out_grads,
    basis_in,
    basis_out,
    eigenvalues,
    damping,
    layer_order,
    query_ids,
    train_ids,
):
    slot_count = basis_in.shape[0]
    layer_groups = lax.axis_size("layer")
    row_count = lax.axis_size("row")
    col_count = lax.axis_size("col")
    ordered_in = jnp.take(activations, layer_order, axis=0)
    ordered_out = jnp.take(out_grads, layer_order, axis=0)
    in_block = ordered_in.shape[1]
    moved_in = lax.all_to_all(ordered_in, "layer", split_axis=0, concat_axis=1, tiled=True)
    shaped_in = moved_in.reshape(slot_count, layer_groups, in_block, moved_in.shape[2])
    joined_in = lax.all_gather(shaped_in, "row", axis=2, tiled=True)
    inputs_full = joined_in.reshape(
        slot_count, layer_groups * row_count * in_block, moved_in.shape[2]
    )
    out_block = ordered_out.shape[1]
    moved_out = lax.all_to_all(ordered_out, "layer", split_axis=0, concat_axis=1, tiled=True)
    shaped_out = moved_out.reshape(slot_count, layer_groups, out_block, moved_out.shape[2])
    joined_out = lax.all_gather(shaped_out, "col", axis=2, tiled=True)
    grads_full = joined_out.reshape(
        slot_count, layer_groups * col_count * out_block, moved_out.shape[2]
    )
    partial_in = jnp.einsum(
        "ltc,lcj->ltj", inputs_full, basis_in, preferred_element_type=jnp.float32
    )
    rotated_in = lax.psum(partial_in.astype(jnp.bfloat16), "col")
    partial_out = jnp.einsum(
        "ltr,lri->lti", grads_full, basis_out, preferred_element_type=jnp.float32
    )
    rotated_out = lax.psum(partial_out.astype(jnp.bfloat16), "row")
    query_tokens = query_ids.shape[0]
    query_mask = (query_ids[None, :] == jnp.arange(QUERIES, dtype=jnp.int32)[:, None]).astype(
        jnp.bfloat16
    )
    train_onehot = (train_ids[:, None] == jnp.arange(TRAIN, dtype=jnp.int32)[None, :]).astype(
        jnp.float32
    )
    query_in = rotated_in[0, :query_tokens]
    query_out = rotated_out[0, :query_tokens]
    train_in = rotated_in[0, query_tokens:]
    train_out = rotated_out[0, query_tokens:]
    masked = query_mask[:, :, None] * query_in[None, :, :]
    query_gram = jnp.einsum("si,qsj->qij", query_out, masked, preferred_element_type=jnp.float32)
    precond = (query_gram / (eigenvalues[0] + damping[0])).astype(jnp.bfloat16)
    mapped = jnp.einsum("ui,qij->quj", train_out, precond, preferred_element_type=jnp.float32)
    values = jnp.sum(mapped * train_in[None, :, :], axis=2)
    total = jnp.dot(values, train_onehot, precision=lax.Precision.HIGHEST)
    return lax.psum(total, ("layer", "col", "row"))


def solution(mesh):
    in_specs = (
        P(None, ("layer", "row"), "col"),
        P(None, ("layer", "col"), "row"),
        P("layer", "col", "row"),
        P("layer", "row", "col"),
        P("layer", "col", "row"),
        P("layer"),
        P(),
        P(),
        P(),
    )
    out_specs = P()
    return jax.shard_map(body, mesh=mesh, in_specs=in_specs, out_specs=out_specs, check_vma=False)
```

profile of v0, /device:TPU:0, one launch (start us, length us, event | category | flops | bytes accessed | tf_op | source)
XLA Modules:
  0.0 537.3 jit_solution(4422896807830578401)
XLA Ops:
  6.5 0.8 compare_and_fusion
  8.0 1.7 gather_fusion
  9.8 1.0 broadcast_select_fusion.1
  10.8 4.3 all-to-all-start
  15.0 2.1 gather_fusion.1
  17.1 3.2 broadcast_select_fusion
  20.3 6.3 %all-to-all-done = bf16[4,96,1024]{2,1,0:T(8,128)(2,1)S(1)} async-done(((bf16[4,96,1024]{2,1,0:T(8,128)(2,1)}), bf16[4,96,1024]{2,1,0:T(8,128)(2,1)S(1)}, u32[]{:S(2)}, u32[]{:S(2)}) %all-to-all-start) | async-done | bytes 786464 | tf_op jit(solution)/shard_map/all_to_all | solution.py:28
  26.7 3.6 all-to-all-start.1
  30.3 0.7 all-gather.5.cloned.1.call-update
  31.1 25.0 %all-to-all-done.1 = bf16[4,48,5504]{2,1,0:T(8,128)(2,1)S(1)} async-done(((bf16[4,48,5504]{2,1,0:T(8,128)(2,1)}), bf16[4,48,5504]{2,1,0:T(8,128)(2,1)S(1)}, u32[]{:S(2)}, u32[]{:S(2)}) %all-to-all-start.1) | async-done | bytes 2113568 | tf_op jit(solution)/shard_map/all_to_all | solution.py:35
  56.1 1.3 copy-done.2
  57.5 4.7 all-gather.5.cloned.1.call-done
  62.2 7.7 %fusion.18 = bf16[1,768,2048]{2,1,0:T(8,128)(2,1)} fusion(bf16[768,1024]{1,0:T(8,128)(2,1)} %bitcast.69, bf16[1,1024,2048]{2,1,0:T(8,128)(2,1)} %param.11), kind=kOutput, calls=%fused_computation.16 | convolution fusion | flops 3222798336 | bytes 8912896 | tf_op jit(solution)/shard_map/ltc,lcj->ltj/dot_general | solution.py:41
  70.2 144.3 %all-gather.7.cloned.1.call-done = bf16[4,192,5504]{2,1,0:T(8,128)(2,1)} async-done(((bf16[4,48,5504]{2,1,0:T(8,128)(2,1)}), bf16[4,192,5504]{2,1,0:T(8,128)(2,1)}) %all-gather.7.cloned.1.call-update) | async-done | bytes 8454160 | tf_op jit(solution)/shard_map/all_gather | solution.py:37
  214.5 31.3 %fusion.8 = bf16[1,768,2752]{1,2,0:T(8,128)(2,1)} fusion(bf16[768,5504]{1,0:T(8,128)(2,1)} %bitcast.68, bf16[1,5504,2752]{1,2,0:T(8,128)(2,1)} %param.12), kind=kOutput, calls=%fused_computation.11 | convolution fusion | flops 23267917824 | bytes 42975232 | tf_op jit(solution)/shard_map/ltr,lri->lti/dot_general | solution.py:45
  246.5 17.0 %add_bitcast_fusion = f32[2752,2048]{1,0:T(8,128)} fusion(f32[1,2752,2048]{2,1,0:T(8,128)} %param.13, f32[]{:T(128)} %bitcast.67), kind=kLoop, calls=%fused_computation.7 | loop fusion | flops 5636096 | bytes 45088772 | tf_op jit(solution)/shard_map/div | solution.py:62
  263.5 72.7 %all-reduce.3.cloned.1.call-done = bf16[1,768,2048]{2,1,0:T(8,128)(2,1)} async-done(((bf16[1,768,2048]{2,1,0:T(8,128)(2,1)}), bf16[1,768,2048]{2,1,0:T(8,128)(2,1)}) %all-reduce.3.cloned.1.call-update) | async-done | bytes 3145744 | tf_op jit(solution)/shard_map/psum | solution.py:44
  336.2 4.1 fusion.21
  340.2 5.4 %copy.12 = f32[512,2048]{0,1:T(8,128)} copy(f32[512,2048]{1,0:T(8,128)} %fusion.21) | data formatting | bytes 8388608 | tf_op jit(solution)/shard_map/mul | solution.py:64
  345.7 1.3 slice_bitcast_fusion.6
  347.0 99.2 %all-reduce.5.cloned.1.call-done = bf16[1,768,2752]{1,2,0:T(8,128)(2,1)} async-done(((bf16[1,768,2752]{1,2,0:T(8,128)(2,1)}), bf16[1,768,2752]{1,2,0:T(8,128)(2,1)}) %all-reduce.5.cloned.1.call-update) | async-done | bytes 4227088 | tf_op jit(solution)/shard_map/psum | solution.py:48
  446.1 3.6 slice_bitcast_fusion.13
  449.7 41.4 %fusion.4 = f32[4,512]{1,0:T(4,128)S(1)} fusion(f32[512,2048]{0,1:T(8,128)} %copy.12, f32[2752,2048]{1,0:T(8,128)} %add_bitcast_fusion, bf16[1,768,2752]{1,2,0:T(8,128)(2,1)} %all-reduce.5.cloned.1.call-done, bf16[256,2048]{1,0:T(8,128)(2,1)S(1)} %slice_bitcast_fusion.6, bf16[4,256]{1,0:T(4,128)(2,1)S(1)} %fusion.28, ...), kind=kOutput, calls=%fused_computation.9 | convolution fusion | flops 34690039808 | bytes 32024576 | tf_op jit(solution)/shard_map/ui,qij->quj/dot_general | solution.py:63
  491.4 39.3 %psum.23 = f32[4,16]{1,0:T(4,128)} all-reduce(f32[4,16]{1,0:T(4,128)S(1)} %fusion.26), channel_id=1, replica_groups=mesh['layer'=4,'col'=4,'row'=2] {'layer','col','row'}, use_global_device_ids=true, to_apply=%region_3.4 | all-reduce | flops 64 | bytes 512 | tf_op jit(solution)/shard_map/psum | solution.py:66
  (22 shorter events, 1.4 us)
Async XLA Ops:
  6.5 8.5 %copy-start = (bf16[4,48,5504]{2,1,0:T(8,128)(2,1)S(1)}, bf16[4,48,5504]{2,1,0:T(8,128)(2,1)}, u32[]{:S(2)}) copy-start(bf16[4,48,5504]{2,1,0:T(8,128)(2,1)} %param.10) | copy-start | bytes 6340612
  10.8 15.9 %all-to-all-start = ((bf16[4,96,1024]{2,1,0:T(8,128)(2,1)}), bf16[4,96,1024]{2,1,0:T(8,128)(2,1)S(1)}, u32[]{:S(2)}, u32[]{:S(2)}) async-start(bf16[4,96,1024]{2,1,0:T(8,128)(2,1)} %broadcast_select_fusion.1), calls=%async_computation | async-start | bytes 1572864 | tf_op jit(solution)/shard_map/all_to_all | solution.py:28
  26.7 3.7 copy-start.3
  26.7 29.4 %all-to-all-start.1 = ((bf16[4,48,5504]{2,1,0:T(8,128)(2,1)}), bf16[4,48,5504]{2,1,0:T(8,128)(2,1)S(1)}, u32[]{:S(2)}, u32[]{:S(2)}) async-start(bf16[4,48,5504]{2,1,0:T(8,128)(2,1)} %broadcast_select_fusion), calls=%async_computation.1 | async-start | bytes 4227072 | tf_op jit(solution)/shard_map/all_to_all | solution.py:35
  30.3 31.9 %all-gather.5.cloned.1.call-start = ((), (), s32[]{:S(2)}) async-start(), calls=%async_computation.4 | async-start | bytes 2359296 | tf_op jit(solution)/shard_map/all_gather | solution.py:30
  31.0 183.5 %all-gather.7.cloned.1.call-start = ((), (), s32[]{:S(2)}) async-start(), calls=%async_computation.5 | async-start | bytes 10567680 | tf_op jit(solution)/shard_map/all_gather | solution.py:37
  56.1 1.3 copy-start.2
  57.5 278.7 %all-reduce.3.cloned.1.call-start = ((), (), s32[]{:S(2)}) async-start(), calls=%async_computation.2 | async-start | bytes 6291456 | tf_op jit(solution)/shard_map/psum | solution.py:44
  70.0 376.1 %all-reduce.5.cloned.1.call-start = ((), (), s32[]{:S(2)}) async-start(), calls=%async_computation.3 | async-start | bytes 8454144 | tf_op jit(solution)/shard_map/psum | solution.py:48
  245.8 0.7 copy-start.4
  449.7 41.5 %copy-start.5 = (s32[512]{0:T(512)S(1)}, s32[512]{0:T(512)}, u32[]{:S(2)}) copy-start(s32[512]{0:T(512)} %param.17) | copy-start | bytes 6148
  449.7 81.0 %copy-start.1 = (bf16[4,48,5504]{2,1,0:T(8,128)(2,1)S(1)}, bf16[4,48,5504]{2,1,0:T(8,128)(2,1)}, u32[]{:S(2)}) copy-start(bf16[4,48,5504]{2,1,0:T(8,128)(2,1)} %param.10) | copy-start | bytes 6340612
Sparse Core Ops, SparseCore 0:
  32.6 29.5 all-gather.4
  63.8 150.6 all-gather.6
  216.9 119.2 all-reduce.2
  338.5 107.6 all-reduce.4
where the time goes:
time: 538 us; the launch traced here: 537 us
  waiting for transfers between devices  353 us (66%)
  matrix products  80.7 us (15%)
  blocking collectives  39.3 us (7%)
  other arithmetic  26.7 us (5%)
  local copies, waits for them, and re-layouts  15.5 us (3%)
  between operations  13.9 us (3%)
  starting transfers between devices  8.21 us (2%)
    all_gather x1, waiting for transfers between devices, body(): joined_out = lax.all_gather(shaped_out, 'col', axis=2, tiled=True)  144 us
    psum x1, waiting for transfers between devices, body(): rotated_out = lax.psum(partial_out.astype(jnp.bfloat16), 'row')  99.2 us
    psum x1, waiting for transfers between devices, body(): rotated_in = lax.psum(partial_in.astype(jnp.bfloat16), 'col')  72.7 us
    dot_general x1, matrix products, body(): jnp.einsum('ui,qij->quj', train_out, precond, preferred_element_type=jnp....  41.4 us
    psum x1, blocking collectives, body(): return lax.psum(total, ('layer', 'col', 'row'))  39.3 us
    dot_general x1, matrix products, body(): jnp.einsum('ltr,lri->lti', grads_full, basis_out, preferred_element_type=...  31.3 us
    all_to_all x1, waiting for transfers between devices, body(): lax.all_to_all(ordered_out, 'layer', split_axis=0, concat_axis=1, tiled=T...  25 us
    div x1, other arithmetic, body(): precond = (query_gram / (eigenvalues[0] + damping[0])).astype(jnp.bfloat16)  17 us
  transfers between devices with their start and end apart: 6, of which 6 were waited for; matrix products, arithmetic and copies ran while one was open for 13% of the time, Pallas kernels for 0%

commit v1 on v0

--- a/solution.py
+++ b/solution.py
@@ -2,6 +2,7 @@
 import jax.numpy as jnp
 from jax import lax
 from jax.sharding import PartitionSpec as P
+from jax.lax import all_gather
 
 QUERIES = 4
 TRAIN = 16
@@ -18,6 +19,11 @@
     query_ids,
     train_ids,
 ):
+
+    def point_rows_on(in_array):
+        left_arr = all_gather(in_array, "row")
+        return jnp.sum(left_arr, axis=0)
+
     slot_count = basis_in.shape[0]
     layer_groups = lax.axis_size("layer")
     row_count = lax.axis_size("row")
@@ -45,7 +51,7 @@
     partial_out = jnp.einsum(
         "ltr,lri->lti", grads_full, basis_out, preferred_element_type=jnp.float32
     )
-    rotated_out = lax.psum(partial_out.astype(jnp.bfloat16), "row")
+    rotated_out = point_rows_on(partial_out.astype(jnp.bfloat16))
     query_tokens = query_ids.shape[0]
     query_mask = (query_ids[None, :] == jnp.arange(QUERIES, dtype=jnp.int32)[:, None]).astype(
         jnp.bfloat16

time: 538 us -> 579 us (1.076)
  other arithmetic: 26.7 us -> 51.8 us
  local copies, waits for them, and re-layouts: 15.5 us -> 33.4 us
    psum x1 -> x0, waiting for transfers between devices: 99.2 us -> none  [body(): rotated_out = lax.psum(partial_out.astype(jnp.bfloat16), 'row')]
    all_gather x0 -> x1, waiting for transfers between devices: none -> 96.6 us  [point_rows_on(): left_arr = all_gather(in_array, 'row')]
    reduce_sum x0 -> x1, other arithmetic: none -> 25 us  [point_rows_on(): return jnp.sum(left_arr, axis=0)]
    all_gather x0 -> x1, local copies, waits for them, and re-layouts: none -> 17.7 us  [point_rows_on(): left_arr = all_gather(in_array, 'row')]
where the time goes in v1:
time: 579 us; the launch traced here: 578 us
  waiting for transfers between devices  350 us (60%)
  matrix products  80.8 us (14%)
  other arithmetic  51.8 us (9%)
  blocking collectives  39.3 us (7%)
  local copies, waits for them, and re-layouts  33.4 us (6%)
  between operations  13.9 us (2%)
  starting transfers between devices  8.21 us (1%)
    all_gather x1, waiting for transfers between devices, body(): joined_out = lax.all_gather(shaped_out, 'col', axis=2, tiled=True)  144 us
    all_gather x1, waiting for transfers between devices, point_rows_on(): left_arr = all_gather(in_array, 'row')  96.6 us
    psum x1, waiting for transfers between devices, body(): rotated_in = lax.psum(partial_in.astype(jnp.bfloat16), 'col')  72.7 us
    dot_general x1, matrix products, body(): jnp.einsum('ui,qij->quj', train_out, precond, preferred_element_type=jnp....  41.4 us
    psum x1, blocking collectives, body(): return lax.psum(total, ('layer', 'col', 'row'))  39.3 us
    dot_general x1, matrix products, body(): jnp.einsum('ltr,lri->lti', grads_full, basis_out, preferred_element_type=...  31.3 us
    reduce_sum x1, other arithmetic, point_rows_on(): return jnp.sum(left_arr, axis=0)  25 us
    all_to_all x1, waiting for transfers between devices, body(): lax.all_to_all(ordered_out, 'layer', split_axis=0, concat_axis=1, tiled=T...  25 us
  transfers between devices with their start and end apart: 6, of which 6 were waited for; matrix products, arithmetic and copies ran while one was open for 13% of the time, Pallas kernels for 0%

profile of v1, /device:TPU:0, one launch (start us, length us, event | category | flops | bytes accessed | tf_op | source)
XLA Modules:
  0.0 577.7 jit_solution(12751348106880920039)
XLA Ops:
  8.0 1.7 gather_fusion
  9.8 1.0 broadcast_select_fusion.1
  10.8 4.3 all-to-all-start
  15.0 2.1 gather_fusion.1
  17.1 3.2 broadcast_select_fusion
  20.3 6.3 %all-to-all-done = bf16[4,96,1024]{2,1,0:T(8,128)(2,1)S(1)} async-done(((bf16[4,96,1024]{2,1,0:T(8,128)(2,1)}), bf16[4,96,1024]{2,1,0:T(8,128)(2,1)S(1)}, u32[]{:S(2)}, u32[]{:S(2)}) %all-to-all-start) | async-done | bytes 786464 | tf_op jit(solution)/shard_map/all_to_all | solution.py:34
  26.7 3.6 all-to-all-start.1
  31.1 25.0 %all-to-all-done.1 = bf16[4,48,5504]{2,1,0:T(8,128)(2,1)S(1)} async-done(((bf16[4,48,5504]{2,1,0:T(8,128)(2,1)}), bf16[4,48,5504]{2,1,0:T(8,128)(2,1)S(1)}, u32[]{:S(2)}, u32[]{:S(2)}) %all-to-all-start.1) | async-done | bytes 2113568 | tf_op jit(solution)/shard_map/all_to_all | solution.py:41
  56.1 1.3 copy-done.2
  57.5 4.7 all-gather.7.cloned.1.call-done
  62.2 7.8 %fusion.15 = bf16[1,768,2048]{2,1,0:T(8,128)(2,1)} fusion(bf16[768,1024]{1,0:T(8,128)(2,1)} %bitcast.70, bf16[1,1024,2048]{2,1,0:T(8,128)(2,1)} %param.11), kind=kOutput, calls=%fused_computation.15 | convolution fusion | flops 3222798336 | bytes 8912896 | tf_op jit(solution)/shard_map/ltc,lcj->ltj/dot_general | solution.py:47
  70.3 144.3 %all-gather.9.cloned.1.call-done = bf16[4,192,5504]{2,1,0:T(8,128)(2,1)} async-done(((bf16[4,48,5504]{2,1,0:T(8,128)(2,1)}), bf16[4,192,5504]{2,1,0:T(8,128)(2,1)}) %all-gather.9.cloned.1.call-update) | async-done | bytes 8454160 | tf_op jit(solution)/shard_map/all_gather | solution.py:43
  214.5 31.3 %fusion.5 = bf16[768,2752]{0,1:T(8,128)(2,1)} fusion(bf16[768,5504]{1,0:T(8,128)(2,1)} %bitcast.69, bf16[1,5504,2752]{1,2,0:T(8,128)(2,1)} %param.12), kind=kOutput, calls=%fused_computation.10 | convolution fusion | flops 23267917824 | bytes 42975232 | tf_op jit(solution)/shard_map/ltr,lri->lti/dot_general | solution.py:51
  246.5 17.0 %add_bitcast_fusion = f32[2752,2048]{1,0:T(8,128)} fusion(f32[1,2752,2048]{2,1,0:T(8,128)} %param.13, f32[]{:T(128)} %bitcast.66), kind=kLoop, calls=%fused_computation.7 | loop fusion | flops 5636096 | bytes 45088772 | tf_op jit(solution)/shard_map/div | solution.py:68
  263.5 72.7 %all-reduce.2.cloned.1.call-done = bf16[1,768,2048]{2,1,0:T(8,128)(2,1)} async-done(((bf16[1,768,2048]{2,1,0:T(8,128)(2,1)}), bf16[1,768,2048]{2,1,0:T(8,128)(2,1)}) %all-reduce.2.cloned.1.call-update) | async-done | bytes 3145744 | tf_op jit(solution)/shard_map/psum | solution.py:50
  336.2 4.1 fusion.18
  340.2 5.4 copy.14
  345.7 1.5 slice_bitcast_fusion.6
  347.2 96.6 %all-gather.11.cloned.1.call-done = bf16[1536,2752]{0,1:T(8,128)(2,1)} async-done(((bf16[768,2752]{0,1:T(8,128)(2,1)}), bf16[1536,2752]{0,1:T(8,128)(2,1)}) %all-gather.11.cloned.1.call-update) | async-done | bytes 8454160 | tf_op jit(solution)/shard_map/all_gather | solution.py:24
  443.8 17.7 %reshape.86 = bf16[2,768,2752]{1,0,2:T(2,128)(2,1)} reshape(bf16[1536,2752]{0,1:T(8,128)(2,1)} %all-gather.11.cloned.1.call-done) | data formatting | bytes 16908288 | tf_op jit(solution)/shard_map/all_gather | solution.py:24
  461.6 25.0 %reduce.2 = bf16[768,2752]{0,1:T(8,128)(2,1)} reduce(bf16[2,768,2752]{1,0,2:T(2,128)(2,1)} %reshape.86, bf16[]{:T(256)} %constant.30.clone.1), dimensions={0}, to_apply=%region_1.2 | reduce | flops 2113536 | bytes 12681218 | tf_op jit(solution)/shard_map/reduce_sum | solution.py:25
  486.6 3.6 slice_bitcast_fusion.13
  490.1 41.4 %fusion.4 = f32[4,512]{1,0:T(4,128)S(1)} fusion(f32[512,2048]{0,1:T(8,128)} %copy.14, f32[2752,2048]{1,0:T(8,128)} %add_bitcast_fusion, bf16[1,768,2752]{1,2,0:T(8,128)(2,1)} %bitcast.68, bf16[256,2048]{1,0:T(8,128)(2,1)S(1)} %slice_bitcast_fusion.6, bf16[4,256]{1,0:T(4,128)(2,1)S(1)} %fusion.25, bf16[512,2752,1]{0,1,2:T(8,128)(2,1)} %slice_bitcast_fusion.13), kind=kOutput, calls=%fused_computation.9 | convolution fusion | flops 34690039808 | bytes 32024576 | tf_op jit(solution)/shard_map/ui,qij->quj/dot_general | solution.py:69
  531.9 39.3 %psum.15 = f32[4,16]{1,0:T(4,128)} all-reduce(f32[4,16]{1,0:T(4,128)S(1)} %fusion.23), channel_id=1, replica_groups=mesh['layer'=4,'col'=4,'row'=2] {'layer','col','row'}, use_global_device_ids=true, to_apply=%region_3.4 | all-reduce | flops 64 | bytes 512 | tf_op jit(solution)/shard_map/psum | solution.py:72
  (24 shorter events, 2.8 us)
Async XLA Ops:
  6.5 8.5 %copy-start = (bf16[4,48,5504]{2,1,0:T(8,128)(2,1)S(1)}, bf16[4,48,5504]{2,1,0:T(8,128)(2,1)}, u32[]{:S(2)}) copy-start(bf16[4,48,5504]{2,1,0:T(8,128)(2,1)} %param.10) | copy-start | bytes 6340612
  10.8 15.9 %all-to-all-start = ((bf16[4,96,1024]{2,1,0:T(8,128)(2,1)}), bf16[4,96,1024]{2,1,0:T(8,128)(2,1)S(1)}, u32[]{:S(2)}, u32[]{:S(2)}) async-start(bf16[4,96,1024]{2,1,0:T(8,128)(2,1)} %broadcast_select_fusion.1), calls=%async_computation | async-start | bytes 1572864 | tf_op jit(solution)/shard_map/all_to_all | solution.py:34
  26.7 3.7 copy-start.3
  26.7 29.4 %all-to-all-start.1 = ((bf16[4,48,5504]{2,1,0:T(8,128)(2,1)}), bf16[4,48,5504]{2,1,0:T(8,128)(2,1)S(1)}, u32[]{:S(2)}, u32[]{:S(2)}) async-start(bf16[4,48,5504]{2,1,0:T(8,128)(2,1)} %broadcast_select_fusion), calls=%async_computation.1 | async-start | bytes 4227072 | tf_op jit(solution)/shard_map/all_to_all | solution.py:41
  30.3 31.9 %all-gather.7.cloned.1.call-start = ((), (), s32[]{:S(2)}) async-start(), calls=%async_computation.3 | async-start | bytes 2359296 | tf_op jit(solution)/shard_map/all_gather | solution.py:36
  31.0 183.5 %all-gather.9.cloned.1.call-start = ((), (), s32[]{:S(2)}) async-start(), calls=%async_computation.4 | async-start | bytes 10567680 | tf_op jit(solution)/shard_map/all_gather | solution.py:43
  56.1 1.3 copy-start.2
  57.4 278.7 %all-reduce.2.cloned.1.call-start = ((), (), s32[]{:S(2)}) async-start(), calls=%async_computation.2 | async-start | bytes 6291456 | tf_op jit(solution)/shard_map/psum | solution.py:50
  70.0 373.8 %all-gather.11.cloned.1.call-start = ((), (), s32[]{:S(2)}) async-start(), calls=%async_computation.5 | async-start | bytes 12681216 | tf_op jit(solution)/shard_map/all_gather | solution.py:24
  245.8 0.7 copy-start.4
  490.1 41.5 %copy-start.5 = (s32[512]{0:T(512)S(1)}, s32[512]{0:T(512)}, u32[]{:S(2)}) copy-start(s32[512]{0:T(512)} %param.17) | copy-start | bytes 6148
  490.1 81.0 %copy-start.1 = (bf16[4,48,5504]{2,1,0:T(8,128)(2,1)S(1)}, bf16[4,48,5504]{2,1,0:T(8,128)(2,1)}, u32[]{:S(2)}) copy-start(bf16[4,48,5504]{2,1,0:T(8,128)(2,1)} %param.10) | copy-start | bytes 6340612
Sparse Core Ops, SparseCore 0:
  32.6 29.5 all-gather.6
  63.8 150.6 all-gather.8
  216.9 119.2 all-reduce.1
  337.6 106.1 all-gather.10
